TPU v7x, 128 devices: a 2x2x16 block of a 8x8x16 slice. The times are simulated.
128 devices in a mesh: mol: 4 (over y, x), pts: 32 (over z, core).
Axes of the slice: x: 2, y: 2, z: 16, core: 2. Of those that a mesh axis runs over, the one named last changes fastest.
The devices are a block of a 8x8x16 slice.
Arguments:
- points_map: bfloat16 [25600, 800], P(('mol', 'pts')), parts along dimension 0, may hold values from -0.21875 to 0.21875
- trial: bfloat16 [25600, 128], P('mol'), parts along dimension 0, may hold values from -6 to 6
- core: bfloat16 [25600, 6400], P(('mol', 'pts')), parts along dimension 0, may hold values from -2 to 4, as said below
- walkers: bfloat16 [3200, 12, 128], P('mol'), parts along dimension 0, may hold values from -6 to 6
- draws: int32 [25600, 12], P(('mol', 'pts')), parts along dimension 0, may hold values from 0 to 3
Outputs:
- new_walkers: bfloat16 [3200, 12, 128], P(('mol', 'pts')), parts along dimension 0
- energy: float32 [48], P('mol'), parts along dimension 0
There are 4 independent parts, one for each index of `mol`. A program takes and returns all parts, laid end to end along the dimension named above; each array names one. Nothing has to cross between parts.
Inputs may be any that keep to these rules, and one draw needn't show every extreme that they name: core is symmetric.
All inputs are finite; a program needn't handle non-finite values.
Results may differ from a plain program's by a relative error of at most 0.018.
Values may be sent and summed in bfloat16 or wider, within the bound.
No kernel may reach another device: no remote copies, remote signals or barrier semaphores. Data moves between devices by JAX's collectives and lax.ppermute only.
A program may use at most 192 MiB of HBM per device.

v0:
```python
import math

import jax
import jax.numpy as jnp
from jax import lax
from jax.sharding import PartitionSpec as P

TAYLOR = 3


GAUSS_NODES = (-2.3344142, -0.7419637, 0.7419637, 2.3344142)
FIELD_STEP = 0.15


def copy_for_each(value, axis):
    copies = jnp.broadcast_to(value, (lax.axis_size(axis), *value.shape))
    return lax.all_to_all(copies, axis, split_axis=0, concat_axis=0, tiled=True)


def joined_along(pieces, dim):
    lengths = list(pieces.shape[1:])
    lengths[dim] *= pieces.shape[0]
    return jnp.moveaxis(pieces, 0, dim).reshape(lengths)


def gathered_copies(value, axis, dim):
    pieces = copy_for_each(value, axis)
    return joined_along(pieces, dim)


def over_copies(value, axis):
    everything = copy_for_each(value, axis)
    return jnp.sum(everything, axis=0)


def node_lookup(draws):
    values = jnp.zeros(draws.shape, jnp.float32)
    for number, node in enumerate(GAUSS_NODES):
        values = values + jnp.where(draws == number, node, 0.0).astype(jnp.float32)
    return values


def body(points_map, trial, core, walkers, draws):
    point_rows = points_map.shape[0]
    orbitals = points_map.shape[1]
    walker_count = walkers.shape[1]
    occupied = walkers.shape[2]
    point_first = lax.axis_index("pts") * point_rows
    trial_here = lax.dynamic_slice_in_dim(trial, point_first, point_rows, 0)
    flat_walkers = walkers.reshape(orbitals, walker_count * occupied)
    orbit = (
        jnp.dot(points_map, flat_walkers, preferred_element_type=jnp.float32)
        .astype(jnp.bfloat16)
        .reshape(point_rows, walker_count, occupied)
    )
    density = (
        jnp.sum(orbit.astype(jnp.float32) * trial_here.astype(jnp.float32)[:, None, :], axis=2)
        / math.sqrt(occupied)
    ).astype(jnp.bfloat16)
    core_block = core
    potential = jnp.dot(
        core_block, gathered_copies(density, "pts", 0), preferred_element_type=jnp.float32
    )
    field = FIELD_STEP * (node_lookup(draws) - FIELD_STEP * potential)
    local_walkers = jnp.moveaxis(orbit, 1, 0)
    shard_piece = lax.all_gather(points_map, "pts", axis=0, tiled=True)
    remote = (
        jnp.dot(shard_piece, flat_walkers, preferred_element_type=jnp.float32)
        .astype(jnp.bfloat16)
        .reshape(shard_piece.shape[0], walker_count, occupied)
    )
    core_block = core.astype(jnp.float32)

    def per_walker(operands):
        left_orb, right_orb = operands
        forward = jnp.dot(left_orb, trial.T, preferred_element_type=jnp.float32)
        backward = jnp.dot(trial_here, right_orb.T, preferred_element_type=jnp.float32)
        return jnp.sum(core_block * forward * backward)

    exchange = lax.map(per_walker, (local_walkers, jnp.moveaxis(remote, 1, 0))) / occupied
    hartree = jnp.sum(density.astype(jnp.float32) * potential, axis=0)
    total_points = point_rows * lax.axis_size("pts")
    energy = over_copies((hartree - exchange) / (2.0 * total_points), "pts")
    own_rows = orbitals // lax.axis_size("pts")
    map_full = lax.all_gather(points_map, "pts", axis=0, tiled=True)
    field_full = gathered_copies(field, "pts", 0)
    own_cols = walker_count * occupied // lax.axis_size("pts")
    col_start = lax.axis_index("pts") * own_cols
    cols_walkers = lax.dynamic_slice_in_dim(flat_walkers, col_start, own_cols, 1)
    walker_ids = (col_start + jnp.arange(own_cols, dtype=jnp.int32)) // occupied
    field_cols = jnp.take(field_full, walker_ids, axis=1)
    running_cols = cols_walkers.astype(jnp.float32)
    term_cols = cols_walkers
    for degree in range(1, TAYLOR + 1):
        current_cols = jnp.dot(map_full, term_cols, preferred_element_type=jnp.float32).astype(
            jnp.bfloat16
        )
        scaled_cols = (field_cols * current_cols.astype(jnp.float32)).astype(jnp.bfloat16)
        summed_cols = jnp.einsum(
            "pi,pc->ic", map_full, scaled_cols, preferred_element_type=jnp.float32
        )
        term_cols = (summed_cols / degree).astype(jnp.bfloat16)
        running_cols = running_cols + term_cols.astype(jnp.float32)
    placed = lax.all_to_all(
        running_cols.astype(jnp.bfloat16), "pts", split_axis=0, concat_axis=1, tiled=True
    )
    return (placed.reshape(own_rows, walker_count, occupied), energy)


def solution(mesh):
    placed = (
        P(("mol", "pts"), None),
        P("mol", None),
        P(("mol", "pts"), None),
        P("mol", None, None),
        P(("mol", "pts"), None),
    )
    return jax.shard_map(
        body,
        mesh=mesh,
        in_specs=placed,
        out_specs=(P(("mol", "pts"), None, None), P("mol")),
        check_vma=False,
    )
```

profile of v0, /device:TPU:70, one launch (start us, length us, event | category | flops | bytes accessed | tf_op | source)
XLA Modules:
  0.0 349.0 jit_solution(5350496346310560887)
XLA Ops:
  8.0 4.4 %copy.54 = bf16[800,12,128]{0,2,1:T(8,128)(2,1)} copy(bf16[800,12,128]{2,0,1:T(8,128)(2,1)} %param.10) | data formatting | bytes 4915200 | tf_op args[3]
  12.4 3.0 convolution_convert_fusion.4
  16.5 42.7 %all_to_all.32 = bf16[32,200,12]{1,2,0:T(8,128)(2,1)S(1)} all-to-all(bf16[32,200,12]{1,2,0:T(8,128)(2,1)S(1)} %broadcast_in_dim.50), channel_id=1, replica_groups=mesh['mol'=4,'pts'=32] {'pts'}, dimensions={0} | all-to-all | bytes 307200 | tf_op jit(solution)/shard_map/all_to_all | solution.py:17
  59.6 2.7 multiply_reduce_fusion.1
  62.3 0.9 broadcast_in_dim.51
  63.2 5.0 %all-to-all-start.1 = ((f32[32,200,12]{1,2,0:T(8,128)}), f32[32,200,12]{1,2,0:T(8,128)S(1)}, u32[]{:S(2)}, u32[]{:S(2)}) async-start(f32[32,200,12]{1,2,0:T(8,128)} %broadcast_in_dim.51), calls=%async_computation.1 | async-start | bytes 1048576 | tf_op jit(solution)/shard_map/all_to_all | solution.py:17
  68.2 4.4 %convert_element_type.124 = f32[200,6400]{1,0:T(8,128)} convert(bf16[200,6400]{1,0:T(8,128)(2,1)} %param.9) | non-fusion elementwise | flops 1280000 | bytes 7680000 | tf_op jit(solution)/shard_map/convert_element_type | solution.py:72
  72.6 1.0 copy.61
  73.7 33.3 %all-to-all-done.1 = f32[32,200,12]{1,2,0:T(8,128)S(1)} async-done(((f32[32,200,12]{1,2,0:T(8,128)}), f32[32,200,12]{1,2,0:T(8,128)S(1)}, u32[]{:S(2)}, u32[]{:S(2)}) %all-to-all-start.1) | async-done | bytes 307232 | tf_op jit(solution)/shard_map/all_to_all | solution.py:17
  107.5 1.0 gather_fusion
  108.5 20.6 %all-gather.2.cloned.1.call-done = bf16[6400,800]{1,0:T(8,128)(2,1)} async-done(((bf16[200,800]{1,0:T(8,128)(2,1)}), bf16[6400,800]{1,0:T(8,128)(2,1)}) %all-gather.2.cloned.1.call-update) | async-done | bytes 10240016 | tf_op jit(solution)/shard_map/all_gather | solution.py:85
  129.1 28.2 %convolution_convert_fusion = bf16[6400,1536]{0,1:T(8,128)(2,1)} fusion(bf16[6400,800]{1,0:T(8,128)(2,1)} %all-gather.2.cloned.1.call-done, bf16[800,1536]{0,1:T(8,128)(2,1)} %bitcast.69), kind=kOutput, calls=%fused_computation.11 | convolution fusion | flops 15738470400 | bytes 32358400 | tf_op jit(solution)/shard_map/dot_general | solution.py:68
  157.4 26.2 %copy.60 = bf16[6400,12,128]{2,0,1:T(8,128)(2,1)} copy(bf16[6400,12,128]{0,2,1:T(8,128)(2,1)} %bitcast.67) | data formatting | bytes 39321600 | tf_op jit(solution)/shard_map/reshape | solution.py:70
  183.5 81.9 %while.10 = (s32[]{:T(128)}, f32[12]{0:T(128)S(1)}, bf16[12,200,128]{2,1,0:T(8,128)(2,1)}, bf16[6400,128]{1,0:T(8,128)(2,1)S(1)}, f32[200,6400]{1,0:T(8,128)}, /...) while((s32[]{:T(128)}, f32[12]{0:T(128)S(1)}, bf16[12,200,128]{2,1,0:T(8,128)(2,1)}, ...), condition=%wide.region_4.5_spmd, body=%wide.region_2.4_spmd.sunk | while | flops 659200000 | bytes 34100372 | solution.py:80
  183.5 2.8 convolution_bitcast_fusion.3
  186.5 3.1 fusion.63
  190.3 2.8 convolution_bitcast_fusion.3
  193.3 3.1 fusion.63
  196.4 0.8 dynamic_update_slice.5
  197.2 2.8 convolution_bitcast_fusion.3
  200.1 3.1 fusion.63
  204.0 2.8 convolution_bitcast_fusion.3
  206.9 3.1 fusion.63
  210.8 2.8 convolution_bitcast_fusion.3
  213.7 3.1 fusion.63
  216.9 0.8 dynamic_update_slice.5
  217.6 2.8 convolution_bitcast_fusion.3
  220.6 3.1 fusion.63
  224.4 2.8 convolution_bitcast_fusion.3
  227.4 3.1 fusion.63
  230.5 0.8 dynamic_update_slice.5
  231.3 2.8 convolution_bitcast_fusion.3
  234.2 3.1 fusion.63
  238.1 2.8 convolution_bitcast_fusion.3
  241.0 3.1 fusion.63
  244.9 2.8 convolution_bitcast_fusion.3
  247.8 3.1 fusion.63
  251.7 2.8 convolution_bitcast_fusion.3
  254.7 3.1 fusion.63
  258.6 2.8 convolution_bitcast_fusion.3
  261.5 3.1 fusion.63
  266.0 9.1 %all-to-all-start.3 = ((f32[32,1,12]{2,1,0:T(1,128)}), f32[32,1,12]{2,1,0:T(1,128)S(1)}, u32[]{:S(2)}, u32[]{:S(2)}) async-start(f32[32,1,12]{2,1,0:T(1,128)} %broadcast_in_dim.53), calls=%async_computation.3 | async-start | bytes 32768 | tf_op jit(solution)/shard_map/all_to_all | solution.py:17
  275.1 12.6 %convolution_convert_fusion.5 = bf16[48,800]{1,0:T(8,128)(2,1)S(1)} fusion(bf16[6400,800]{1,0:T(8,128)(2,1)} %all-gather.2.cloned.1.call-done, f32[48,6400]{1,0:T(8,128)S(1)} %gather_fusion, pred[48]{0:T(512)(128)(4,1)S(1)} %compare_and_fusion, bf16[800,1536]{0,1:T(8,128)(2,1)} %bitcast.70, s32[]{:T(128)S(6)} %select_n.54), kind=kOutput, calls=%fused_computation.34 | convolution fusion | flops 984614400 | bytes 24329268 | tf_op jit(solution)/shard_map/pi,pc->ic/dot_general | solution.py:99
  287.7 12.6 %fusion.17 = bf16[48,800]{1,0:T(8,128)(2,1)S(1)} fusion(bf16[6400,800]{1,0:T(8,128)(2,1)} %all-gather.2.cloned.1.call-done, bf16[48,800]{1,0:T(8,128)(2,1)S(1)} %convolution_convert_fusion.5, f32[48,6400]{1,0:T(8,128)S(1)} %gather_fusion, pred[48]{0:T(512)(128)(4,1)S(1)} %compare_and_fusion), kind=kOutput, calls=%fused_computation.28 | convolution fusion | flops 984652800 | bytes 11622448 | tf_op jit(solution)/shard_map/pi,pc->ic/dot_general | solution.py:99
  300.3 12.6 %fusion.22 = bf16[800,48]{0,1:T(8,128)(2,1)S(1)} fusion(bf16[6400,800]{1,0:T(8,128)(2,1)} %all-gather.2.cloned.1.call-done, bf16[48,800]{1,0:T(8,128)(2,1)S(1)} %fusion.17, f32[48,6400]{1,0:T(8,128)S(1)} %gather_fusion, pred[48]{0:T(512)(128)(4,1)S(1)} %compare_and_fusion, bf16[48,800]{1,0:T(8,128)(2,1)S(1)} %convolution_convert_fusion.5, ...), kind=kOutput, calls=%fused_computation.33 | convolution fusion | flops 984960000 | bytes 24587780 | tf_op jit(solution)/shard_map/pi,pc->ic/dot_general | solution.py:99
  313.1 1.0 reshape.111
  314.1 12.2 %all-to-all-start.2 = ((bf16[32,2,600]{2,1,0:T(2,128)(2,1)}), bf16[32,2,600]{2,1,0:T(2,128)(2,1)S(1)}, u32[]{:S(2)}, u32[]{:S(2)}) async-start(bf16[32,2,600]{2,1,0:T(2,128)(2,1)} %reshape.111), calls=%async_computation.2 | async-start | bytes 163840 | tf_op jit(solution)/shard_map/all_to_all | solution.py:104
  326.9 13.8 %all-to-all-done.2 = bf16[32,2,600]{2,1,0:T(2,128)(2,1)S(1)} async-done(((bf16[32,2,600]{2,1,0:T(2,128)(2,1)}), bf16[32,2,600]{2,1,0:T(2,128)(2,1)S(1)}, u32[]{:S(2)}, u32[]{:S(2)}) %all-to-all-start.2) | async-done | bytes 76832 | tf_op jit(solution)/shard_map/all_to_all | solution.py:104
  (101 shorter events, 14.0 us)
Async XLA Ops:
  7.2 5.3 %copy-start.1 = (bf16[200,800]{1,0:T(8,128)(2,1)S(1)}, bf16[200,800]{1,0:T(8,128)(2,1)}, u32[]{:S(2)}) copy-start(bf16[200,800]{1,0:T(8,128)(2,1)} %param.7) | copy-start | bytes 960004
  7.2 121.9 %all-gather.2.cloned.1.call-start = ((), (), s32[]{:S(2)}) async-start(), calls=%async_computation.4 | async-start | bytes 11827200 | tf_op jit(solution)/shard_map/all_gather | solution.py:85
  12.4 3.4 copy-start
  15.4 44.2 %copy-start.2 = (s32[200,12]{0,1:T(8,128)S(1)}, s32[200,12]{0,1:T(8,128)}, u32[]{:S(2)}) copy-start(s32[200,12]{0,1:T(8,128)} %param.11) | copy-start | bytes 28804
  63.2 43.8 %all-to-all-start.1 = ((f32[32,200,12]{1,2,0:T(8,128)}), f32[32,200,12]{1,2,0:T(8,128)S(1)}, u32[]{:S(2)}, u32[]{:S(2)}) async-start(f32[32,200,12]{1,2,0:T(8,128)} %broadcast_in_dim.51), calls=%async_computation.1 | async-start | bytes 1048576 | tf_op jit(solution)/shard_map/all_to_all | solution.py:17
  183.5 2.8 slice-start
  183.5 2.9 slice-start.1
  190.3 2.8 slice-start
  190.3 2.9 slice-start.1
  197.2 2.8 slice-start
  197.2 2.9 slice-start.1
  204.0 2.8 slice-start
  204.0 2.9 slice-start.1
  210.8 2.8 slice-start
  210.8 2.9 slice-start.1
  217.6 2.8 slice-start
  217.6 2.9 slice-start.1
  224.4 2.8 slice-start
  224.4 2.9 slice-start.1
  231.3 2.8 slice-start
  231.3 2.9 slice-start.1
  238.1 2.8 slice-start
  238.1 2.9 slice-start.1
  244.9 2.8 slice-start
  244.9 2.9 slice-start.1
  251.7 2.8 slice-start
  251.7 2.9 slice-start.1
  258.5 2.8 slice-start
  258.6 2.9 slice-start.1
  266.0 48.1 %all-to-all-start.3 = ((f32[32,1,12]{2,1,0:T(1,128)}), f32[32,1,12]{2,1,0:T(1,128)S(1)}, u32[]{:S(2)}, u32[]{:S(2)}) async-start(f32[32,1,12]{2,1,0:T(1,128)} %broadcast_in_dim.53), calls=%async_computation.3 | async-start | bytes 32768 | tf_op jit(solution)/shard_map/all_to_all | solution.py:17
  314.1 26.6 %all-to-all-start.2 = ((bf16[32,2,600]{2,1,0:T(2,128)(2,1)}), bf16[32,2,600]{2,1,0:T(2,128)(2,1)S(1)}, u32[]{:S(2)}, u32[]{:S(2)}) async-start(bf16[32,2,600]{2,1,0:T(2,128)(2,1)} %reshape.111), calls=%async_computation.2 | async-start | bytes 163840 | tf_op jit(solution)/shard_map/all_to_all | solution.py:104
Sparse Core Ops, SparseCore 0:
  9.7 119.3 all-gather.1
where the time goes:
time: 351 us; the launch traced here: 349 us
  matrix products  143 us (41%)
  waiting for transfers between devices  68.5 us (20%)
  local copies, waits for them, and re-layouts  48.7 us (14%)
  blocking collectives  42.7 us (12%)
  starting transfers between devices  26.4 us (8%)
  between operations  14.2 us (4%)
  other arithmetic  5.57 us (2%)
    all_to_all x1, blocking collectives, copy_for_each(): return lax.all_to_all(copies, axis, split_axis=0, concat_axis=0, tiled=True)  42.7 us
    dot_general x3, matrix products, body(): jnp.einsum('pi,pc->ic', map_full, scaled_cols, preferred_element_type=jnp...  37.8 us
    dot_general x12, matrix products, per_walker(): forward = jnp.dot(left_orb, trial.T, preferred_element_type=jnp.float32)  37.5 us
    dot_general x12, matrix products, per_walker(): jnp.dot(trial_here, right_orb.T, preferred_element_type=jnp.float32)  33.6 us
    all_to_all x2, waiting for transfers between devices, copy_for_each(): return lax.all_to_all(copies, axis, split_axis=0, concat_axis=0, tiled=True)  33.3 us
    dot_general x1, matrix products, body(): jnp.dot(shard_piece, flat_walkers, preferred_element_type=jnp.float32)  28.2 us
    reshape x1, local copies, waits for them, and re-layouts, body(): remote = jnp.dot(shard_piece, flat_walkers, preferred_element_type=jnp.fl...  26.2 us
    all_gather x1, waiting for transfers between devices, body(): map_full = lax.all_gather(points_map, 'pts', axis=0, tiled=True)  20.6 us
  transfers between devices with their start and end apart: 4, of which 3 were waited for; matrix products, arithmetic and copies ran while one was open for 17% of the time, Pallas kernels for 0%

commit v1 on v0

v1 whole, which is shorter than its diff:
```python
import functools
import math

import jax
import jax.numpy as jnp
from jax import lax
from jax.experimental import pallas as pl
from jax.experimental.pallas import tpu as pltpu
from jax.sharding import PartitionSpec as P

TAYLOR = 3
GAUSS_NODES = (-2.3344142, -0.7419637, 0.7419637, 2.3344142)
FIELD_STEP = 0.15
BF16, F32 = jnp.bfloat16, jnp.float32
NT = (((1,), (1,)), ((), ()))
NN = (((1,), (0,)), ((), ()))
VMEM_LIMIT = 24 * 1024 * 1024


def mm(a, b, dims=NN):
    return lax.dot_general(a, b, dims, preferred_element_type=F32)


def node_lookup(draws):
    values = jnp.zeros(draws.shape, F32)
    for number, node in enumerate(GAUSS_NODES):
        values = values + jnp.where(draws == number, node, 0.0).astype(F32)
    return values


def vmem():
    return pl.BlockSpec(memory_space=pltpu.VMEM)


def cost(flops, moved):
    return pl.CostEstimate(flops=int(flops), bytes_accessed=int(moved), transcendentals=0)


def params():
    return pltpu.CompilerParams(vmem_limit_bytes=VMEM_LIMIT)


def smem():
    return pl.BlockSpec(memory_space=pltpu.SMEM)


def orbit_kernel(occupied, where_ref, own_ref, mate_ref, w_ref, trial_ref, orbit_ref, near_ref, sent_ref):
    rows = own_ref.shape[0]
    x = jnp.concatenate([own_ref[...].astype(F32), mate_ref[...].astype(F32)], axis=0).astype(BF16)
    trial = trial_ref[where_ref[0]].astype(F32)
    near = jnp.concatenate([trial, trial_ref[where_ref[1]].astype(F32)], axis=0)
    near_ref[...] = near.astype(BF16)
    lane = lax.broadcasted_iota(jnp.int32, (rows, 128), 1)
    density = jnp.zeros((rows, 128), F32)
    for pair in range(w_ref.shape[0] // (2 * occupied)):
        both = mm(x, w_ref[pair * 2 * occupied : (pair + 1) * 2 * occupied], NT).astype(BF16)
        for half in range(2):
            one = both[:, half * occupied : (half + 1) * occupied]
            walker = 2 * pair + half
            orbit_ref[walker] = one
            total = jnp.sum(one.astype(F32)[:rows] * trial, axis=1, keepdims=True)
            density = jnp.where(lane == walker, total / math.sqrt(occupied), density)
    turned = density.T[: sent_ref.shape[1]].astype(BF16)
    for device in range(sent_ref.shape[0]):
        sent_ref[device] = turned


def orbit_call(where, own, mate, turned_walkers, trial_blocks):
    rows, orbitals = own.shape
    devices, _, occupied = trial_blocks.shape
    walkers = turned_walkers.shape[0] // occupied
    return pl.pallas_call(
        functools.partial(orbit_kernel, occupied),
        out_shape=(
            jax.ShapeDtypeStruct((walkers, 2 * rows, occupied), BF16),
            jax.ShapeDtypeStruct((2 * rows, occupied), BF16),
            jax.ShapeDtypeStruct((devices, -(-walkers // 16) * 16, rows), BF16),
        ),
        in_specs=[smem()] + [vmem()] * 4,
        out_specs=(vmem(), vmem(), vmem()),
        compiler_params=params(),
        cost_estimate=cost(4 * rows * orbitals * walkers * occupied, 6e6),
        name="orbit",
    )(where, own, mate, turned_walkers, trial_blocks)


def split_kernel(where_ref, core_ref, keep_ref, away_ref):
    width = keep_ref.shape[2]
    odd = where_ref[2] == 1
    for chip in range(keep_ref.shape[0]):
        even_block = core_ref[:, 2 * chip * width : (2 * chip + 1) * width]
        odd_block = core_ref[:, (2 * chip + 1) * width : (2 * chip + 2) * width]
        keep_ref[chip] = jnp.where(odd, odd_block, even_block)
        away_ref[chip] = jnp.where(odd, even_block, odd_block)


def split_call(where, core, width):
    rows, columns = core.shape
    shape = jax.ShapeDtypeStruct((columns // width // 2, rows, width), BF16)
    return pl.pallas_call(
        split_kernel,
        out_shape=(shape, shape),
        in_specs=[smem(), vmem()],
        out_specs=(vmem(), vmem()),
        compiler_params=params(),
        cost_estimate=cost(1e6, 6e6),
        name="split",
    )(where, core)


def field_kernel(walkers, occupied, columns, where_ref, density_ref, keep_ref, away_ref, draws_ref, out_ref, hartree_ref):
    parity = where_ref[2]
    total = None
    for chip in range(keep_ref.shape[0]):
        for block, slot in ((keep_ref, parity), (away_ref, 1 - parity)):
            piece = mm(density_ref[2 * chip + slot], block[chip], NT)
            total = piece if total is None else total + piece
    mine = density_ref[where_ref[0]].astype(F32)
    hartree_ref[...] = jnp.broadcast_to(jnp.sum(mine * total, axis=1, keepdims=True), hartree_ref.shape)
    field = FIELD_STEP * (node_lookup(draws_ref[...]) - FIELD_STEP * total[:walkers])
    for chip in range(out_ref.shape[0]):
        first = columns * chip // occupied
        out_ref[chip, 0:1] = field[first : first + 1]
        second = min(first + 1, walkers - 1)
        out_ref[chip, 1:2] = field[second : second + 1]


def field_call(where, densities, keep, away, draws, occupied, columns):
    devices, padded, rows = densities.shape
    chips = keep.shape[0]
    walkers = draws.shape[0]
    return pl.pallas_call(
        functools.partial(field_kernel, walkers, occupied, columns),
        out_shape=(
            jax.ShapeDtypeStruct((chips, 2, rows), F32),
            jax.ShapeDtypeStruct((padded, 128), F32),
        ),
        in_specs=[smem()] + [vmem()] * 4,
        out_specs=(vmem(), vmem()),
        compiler_params=params(),
        cost_estimate=cost(4e9, 4e6),
        name="field",
    )(where, densities, keep, away, draws)


def exchange_kernel(
    occupied, weight, chunks, where_ref, upper_ref, lower_ref, near_ref, before_ref, w_hbm, orbit_hbm, trial_hbm,
    keep_hbm, came_hbm, out_ref, w_ref, orbit_ref, trial_ref, keep_ref, came_ref, core_ref, far_ref,
    forward_ref, backward_ref, sems,
):
    chip = where_ref[0]
    span = w_ref.shape[0] // chunks
    copies = [
        pltpu.make_async_copy(w_hbm.at[pl.ds(c * span, span)], w_ref.at[pl.ds(c * span, span)], sems.at[c])
        for c in range(chunks)
    ]
    copies += [
        pltpu.make_async_copy(keep_hbm.at[chip], keep_ref, sems.at[chunks]),
        pltpu.make_async_copy(came_hbm.at[chip], came_ref, sems.at[chunks + 1]),
        pltpu.make_async_copy(trial_hbm.at[where_ref[1]], trial_ref, sems.at[chunks + 2]),
        pltpu.make_async_copy(orbit_hbm, orbit_ref, sems.at[chunks + 3]),
    ]
    for copy in copies:
        copy.start()
    x = jnp.concatenate([upper_ref[...], lower_ref[...]], axis=0)
    rows = x.shape[0]
    for c in range(chunks):
        copies[c].wait()
        far_ref[c * span : (c + 1) * span] = mm(w_ref[c * span : (c + 1) * span], x, NT).astype(BF16)
    for copy in copies[chunks:]:
        copy.wait()
    core_ref[:rows] = keep_ref[...].astype(F32)
    core_ref[rows:] = came_ref[...].astype(F32)
    far_trial = trial_ref[...]
    walkers = out_ref.shape[0]
    forward_ref[1] = jnp.zeros(core_ref.shape, F32)
    backward_ref[1] = jnp.zeros(core_ref.shape, F32)

    def gather(walker, slot):
        value = forward_ref[slot] * backward_ref[slot] * core_ref[...]
        total = jnp.sum(value.reshape(-1, 8, rows), axis=0)
        out_ref[walker] = before_ref[walker] + weight * total

    def spread(walker, slot):
        orbit_far = far_ref[pl.ds(pl.multiple_of(walker * occupied, occupied), occupied)]
        forward_ref[slot] = mm(orbit_ref[walker], far_trial, NT)
        backward_ref[slot] = mm(near_ref[...], orbit_far)

    def two(number, carry):
        gather(lax.rem(2 * number + walkers - 1, walkers), 1)
        spread(2 * number, 0)
        gather(2 * number, 0)
        spread(2 * number + 1, 1)
        return carry

    lax.fori_loop(0, walkers // 2, two, 0)
    gather(walkers - 1, 1)


def exchange_call(where, block, turned_walkers, orbit, near, trial_blocks, keep, came, before, weight):
    walkers, near_rows, occupied = orbit.shape
    rows = keep.shape[1]
    wide, orbitals = turned_walkers.shape
    chunks = 3
    return pl.pallas_call(
        functools.partial(exchange_kernel, occupied, weight, chunks),
        out_shape=jax.ShapeDtypeStruct(before.shape, F32),
        in_specs=[smem()] + [vmem()] * 4 + [pl.BlockSpec(memory_space=pl.ANY)] * 5,
        out_specs=vmem(),
        scratch_shapes=[
            pltpu.VMEM((wide, orbitals), BF16),
            pltpu.VMEM(orbit.shape, BF16),
            pltpu.VMEM((rows, occupied), BF16),
            pltpu.VMEM((rows, rows), BF16),
            pltpu.VMEM((rows, rows), BF16),
            pltpu.VMEM((near_rows, rows), F32),
            pltpu.VMEM((wide, rows), BF16),
            pltpu.VMEM((2, near_rows, rows), F32),
            pltpu.VMEM((2, near_rows, rows), F32),
            pltpu.SemaphoreType.DMA((chunks + 4,)),
        ],
        compiler_params=params(),
        cost_estimate=cost(2 * rows * wide * (orbitals + 4 * rows), 5e6),
        name="exchange",
    )(where, *block, near, before, turned_walkers, orbit, trial_blocks, keep, came)


def energy_row(walkers, occupied, shift, partial_ref, hartree_ref, points):
    exchange = jnp.sum(jnp.sum(partial_ref[...], axis=1), axis=1, keepdims=True) / occupied
    energy = (hartree_ref[:walkers] - exchange) / (2.0 * points)
    row = lax.broadcasted_iota(jnp.int32, energy.shape, 0)
    lane = lax.broadcasted_iota(jnp.int32, energy.shape, 1)
    return jnp.sum(jnp.where(lane == row + shift, energy, 0.0), axis=0, keepdims=True)


def step_term(degree, own_ref, other_ref, running_ref):
    columns = running_ref.shape[0]
    term = ((own_ref[:columns] + other_ref[:columns]) / degree).astype(BF16)
    return term, running_ref[...] + term.astype(F32)


def degree_kernel(count, degree, occupied, where_ref, field_ref, *refs):
    blocks, refs = refs[: 2 * count], refs[2 * count :]
    refs, map_ref, sems = refs[:-2], refs[-2], refs[-1]
    copies = []
    for number in range(count):
        cut = blocks[2 * number].shape[0]
        for half, part in enumerate((pl.ds(0, cut), pl.ds(cut, map_ref.shape[1] - cut))):
            copy = pltpu.make_async_copy(
                blocks[2 * number + half], map_ref.at[number, part], sems.at[2 * number + half]
            )
            copy.start()
            copies.append(copy)
    if degree == 1:
        walkers_ref, partial_ref, hartree_ref, out_ref, running_ref = refs
        columns = walkers_ref.shape[0]
        term = walkers_ref[...]
        running_ref[...] = term.astype(F32)
        points = 2 * count * field_ref.shape[2]
        row = energy_row(partial_ref.shape[0], occupied, columns, partial_ref, hartree_ref, points)
        out_ref[columns:, :128] = jnp.broadcast_to(row, (8, 128))
    else:
        own_ref, other_ref, before_ref, out_ref, running_ref = refs
        columns = before_ref.shape[0]
        term, running = step_term(degree - 1, own_ref, other_ref, before_ref)
        running_ref[...] = running
    first = where_ref[count]
    total = None
    for number in range(count):
        copies[2 * number].wait()
        copies[2 * number + 1].wait()
        x = map_ref[number]
        current = mm(term, x, NT).astype(BF16).astype(F32)
        field = field_ref[where_ref[number]]
        column = lax.broadcasted_iota(jnp.int32, current.shape, 0)
        scaled = jnp.where(column < first, field[0:1], field[1:2]) * current
        piece = mm(scaled.astype(BF16), x)
        total = piece if total is None else total + piece
    out_ref[:columns] = total


def degree_call(where, fields, blocks, degree, occupied, columns, *rest):
    count = len(blocks)
    rows, orbitals = fields.shape[2], blocks[0][0].shape[1]
    flat = [piece for block in blocks for piece in block]
    return pl.pallas_call(
        functools.partial(degree_kernel, count, degree, occupied),
        out_shape=(
            jax.ShapeDtypeStruct((columns + 8 if degree == 1 else columns, orbitals), F32),
            jax.ShapeDtypeStruct((columns, orbitals), F32),
        ),
        in_specs=[smem(), vmem()]
        + [pl.BlockSpec(memory_space=pl.ANY)] * len(flat)
        + [vmem()] * len(rest),
        out_specs=(vmem(), vmem()),
        scratch_shapes=[
            pltpu.VMEM((count, rows, orbitals), BF16),
            pltpu.SemaphoreType.DMA((2 * count,)),
        ],
        compiler_params=params(),
        cost_estimate=cost(4 * rows * count * orbitals * columns, 6e6),
        name="degree",
    )(where, fields, *flat, *rest)


def finish_kernel(where_ref, own_ref, other_ref, before_ref, own_energy, other_energy, out_ref, turned_ref):
    columns, orbitals = before_ref.shape
    chips, own_rows, lanes = out_ref.shape
    parity = where_ref[2]
    _, running = step_term(TAYLOR, own_ref, other_ref, before_ref)
    padded = jnp.concatenate([running, jnp.zeros((lanes - columns, orbitals), F32)], axis=0)
    turned_ref[...] = padded.T
    energy = own_energy[:, :lanes] + other_energy[:, :lanes]
    top = energy.astype(BF16).astype(F32)
    middle = (energy - top).astype(BF16).astype(F32)
    low = energy - top - middle
    row = lax.broadcasted_iota(jnp.int32, (own_rows, lanes), 0)
    lane = lax.broadcasted_iota(jnp.int32, (own_rows, lanes), 1)
    extra = jnp.where(row == 0, top[0:1], jnp.where(row == 1, middle[0:1], jnp.where(row == 2, low[0:1], 0.0)))
    for chip in range(chips):
        mine = turned_ref[pl.ds((2 * chip + parity) * own_rows, own_rows)]
        out_ref[chip] = jnp.where(lane < columns, mine, extra).astype(BF16)


def finish_call(where, own, other, running, own_energy, other_energy, devices):
    columns, orbitals = running.shape
    return pl.pallas_call(
        finish_kernel,
        out_shape=jax.ShapeDtypeStruct((devices // 2, orbitals // devices, 128), BF16),
        in_specs=[smem()] + [vmem()] * 5,
        out_specs=vmem(),
        scratch_shapes=[pltpu.VMEM((orbitals, 128), F32)],
        compiler_params=params(),
        cost_estimate=cost(1e6, 2e6),
        name="finish",
    )(where, own, other, running, own_energy, other_energy)


def body(points_map, trial, core, walkers, draws):
    rows, orbitals = points_map.shape
    walker_count, occupied = walkers.shape[1:]
    devices = lax.axis_size("pts")
    chips = devices // 2
    me = lax.axis_index("pts")
    chip, parity = me // 2, me % 2
    swapped = [(i, i ^ 1) for i in range(devices)]
    forward = [(i, (i + 2) % devices) for i in range(devices)]
    backward = [(i, (i - 2) % devices) for i in range(devices)]
    same_core = [[2 * z + c for z in range(chips)] for c in range(2)]
    columns = walker_count * occupied // chips
    cut = rows // 2 // 16 * 16

    def swap(value):
        return lax.ppermute(value, "pts", swapped)

    own = (points_map[:cut], points_map[cut:])
    right, left = own, own
    blocks, offsets = [own], [0]

    def advance(right, left):
        right = tuple(lax.ppermute(piece, "pts", forward) for piece in right)
        left = tuple(lax.ppermute(piece, "pts", backward) for piece in left)
        return right, left

    mate = swap(points_map)
    place = jnp.stack([me, me ^ 1, parity]).astype(jnp.int32)
    turned = walkers.reshape(orbitals, walker_count * occupied).T
    trial_blocks = trial.reshape(devices, rows, occupied)
    orbit, near, sent = orbit_call(place, points_map, mate, turned, trial_blocks)
    densities = lax.all_to_all(sent, "pts", split_axis=0, concat_axis=0, tiled=True)
    keep, away = split_call(place, core, rows)
    came = swap(away)
    outgoing, hartree = field_call(place, densities, keep, away, draws.T, occupied, columns)
    fields = lax.all_to_all(
        outgoing, "pts", split_axis=0, concat_axis=0, tiled=True, axis_index_groups=same_core
    )

    def exchange(offset, block, before, weight):
        far = (chip + offset) % chips
        where = jnp.stack([far, 2 * far + parity]).astype(jnp.int32)
        return exchange_call(
            where, block, turned, orbit, near, trial_blocks, keep, came, before, weight
        )

    def held(pieces, partial):
        out = []
        for piece in pieces:
            piece, partial = lax.optimization_barrier((piece, partial))
            out.append(piece)
        return tuple(out), partial

    partial = jnp.zeros((walker_count, 8, rows), F32)
    half = chips // 2
    pending = (0, own, 1.0)
    for step in range(1, half):
        if step > 2:
            right, partial = held(right, partial)
            left, partial = held(left, partial)
        right, left = advance(right, left)
        partial = exchange(pending[0], pending[1], partial, pending[2])
        blocks += [right, left]
        offsets += [-step, step]
        pending = (-step, right, 2.0) if step % 2 else (step, left, 2.0)
    right, partial = held(right, partial)
    left, partial = held(left, partial)
    far_block = (lax.ppermute(right[0], "pts", forward), lax.ppermute(left[1], "pts", backward))
    partial = exchange(pending[0], pending[1], partial, pending[2])
    blocks.append(far_block)
    offsets.append(half)
    partial = exchange(half, far_block, partial, 1.0)

    start = chip * columns
    first_count = occupied - start % occupied
    sources = (chip + jnp.asarray(offsets, jnp.int32)) % chips
    where = jnp.concatenate([sources, first_count.reshape(1)]).astype(jnp.int32)
    term = lax.dynamic_slice_in_dim(turned, start, columns, 0)
    mine, running = degree_call(
        where, fields, blocks, 1, occupied, columns, term, partial, hartree
    )
    theirs = swap(mine)
    energies = (mine[columns:], theirs[columns:])
    for degree in range(2, TAYLOR + 1):
        mine, running = degree_call(
            where, fields, blocks, degree, occupied, columns, mine, theirs, running
        )
        theirs = swap(mine)
    message = finish_call(place, mine, theirs, running, *energies, devices)
    arrived = lax.all_to_all(
        message, "pts", split_axis=0, concat_axis=0, tiled=True, axis_index_groups=same_core
    )
    new_walkers = jnp.moveaxis(arrived[:, :, :columns], 0, 1)
    new_walkers = new_walkers.reshape(orbitals // devices, walker_count, occupied)
    energy = jnp.sum(arrived[:, :3, columns : columns + walker_count].astype(F32), axis=(0, 1))
    return (new_walkers, energy)


def solution(mesh):
    placed = (
        P(("mol", "pts"), None),
        P("mol", None),
        P(("mol", "pts"), None),
        P("mol", None, None),
        P(("mol", "pts"), None),
    )
    return jax.shard_map(
        body,
        mesh=mesh,
        in_specs=placed,
        out_specs=(P(("mol", "pts"), None, None), P("mol")),
        check_vma=False,
    )
```

time: 351 us -> 273 us (0.78)
  matrix products: 143 us -> 0 us
  Pallas kernels: 0 us -> 107 us
  waiting for transfers between devices: 68.5 us -> 5.6 us
  starting transfers between devices: 26.4 us -> 87.6 us
  blocking collectives: 42.7 us -> 26.4 us
  between operations: 14.2 us -> 1.63 us
  local copies, waits for them, and re-layouts: 48.7 us -> 39.6 us
  other arithmetic: 5.57 us -> 2.02 us
    dot_general x30 -> x0, matrix products: 143 us -> none  [the longest x3 37.8 us: body(): jnp.einsum('pi,pc->ic', map_full, scaled_cols, preferred_element_type=jnp...]
    pallas_call x0 -> x16, Pallas kernels: none -> 107 us  [the longest x9 58.3 us: exchange_call(): pl.pallas_call(functools.partial(exchange_kernel, occupied, weight, chunk...]
    ppermute x0 -> x35, starting transfers between devices: none -> 67.7 us  [the longest x14 46.3 us: advance(): left = tuple((lax.ppermute(piece, 'pts', backward) for piece in left))]
    all_to_all x3 -> x2, waiting for transfers between devices: 47.2 us -> 0.01 us  [the longest x1 0.01 us: body(): lax.all_to_all(sent, 'pts', split_axis=0, concat_axis=0, tiled=True)]
    unnamed x10 -> x120, local copies, waits for them, and re-layouts: 6.53 us -> 36.8 us
    reshape x5 -> x1, local copies, waits for them, and re-layouts: 27.4 us -> 0.13 us  [body(): new_walkers.reshape(orbitals // devices, walker_count, occupied)]
    all_gather x1 -> x0, waiting for transfers between devices: 20.6 us -> none  [body(): map_full = lax.all_gather(points_map, 'pts', axis=0, tiled=True)]
    all_to_all x1, blocking collectives: 42.7 us -> 26.4 us  [body(): lax.all_to_all(message, 'pts', split_axis=0, concat_axis=0, tiled=True, a...]
  transfers between devices with their start and end apart: 4 -> 37, of which waited for: 3 -> 6; matrix products, arithmetic and copies ran while one was open for 17% -> 3% of each run, Pallas kernels for 0% -> 24%
where the time goes in v1:
time: 273 us; the launch traced here: 270 us
  Pallas kernels  107 us (39%)
  starting transfers between devices  87.6 us (32%)
  local copies, waits for them, and re-layouts  39.6 us (15%)
  blocking collectives  26.4 us (10%)
  waiting for transfers between devices  5.6 us (2%)
    pallas_call x9, Pallas kernels, exchange_call(): pl.pallas_call(functools.partial(exchange_kernel, occupied, weight, chunk...  58.3 us
    ppermute x14, starting transfers between devices, advance(): left = tuple((lax.ppermute(piece, 'pts', backward) for piece in left))  46.3 us
    pallas_call x3, Pallas kernels, degree_call(): pl.pallas_call(functools.partial(degree_kernel, count, degree, occupied),...  37.2 us
    unnamed x120, local copies, waits for them, and re-layouts  36.8 us
    all_to_all x1, blocking collectives, body(): lax.all_to_all(message, 'pts', split_axis=0, concat_axis=0, tiled=True, a...  26.4 us
    ppermute x14, starting transfers between devices, advance(): right = tuple((lax.ppermute(piece, 'pts', forward) for piece in right))  17.2 us
    all_to_all x1, starting transfers between devices, body(): lax.all_to_all(outgoing, 'pts', split_axis=0, concat_axis=0, tiled=True,...  11.6 us
    all_to_all x1, starting transfers between devices, body(): lax.all_to_all(sent, 'pts', split_axis=0, concat_axis=0, tiled=True)  8.29 us
  transfers between devices with their start and end apart: 37, of which 6 were waited for; matrix products, arithmetic and copies ran while one was open for 3% of the time, Pallas kernels for 24%

profile of v1, /device:TPU:70, one launch (start us, length us, event | category | flops | bytes accessed | tf_op | source)
XLA Modules:
  0.0 270.1 jit_solution(17708652827313874659)
XLA Ops:
  0.7 1.7 copy-done.31
  2.4 5.6 %split.1 = (bf16[16,200,200]{2,1,0:T(8,128)(2,1)S(1)}, bf16[16,200,200]{2,1,0:T(8,128)(2,1)}) custom-call(s32[3]{0:T(128)S(1)} %pad_add_fusion.where_ref, bf16[200,6400]{1,0:T(8,128)(2,1)S(1)} %copy-done.31), custom_call_target="tpu_custom_call" | custom-call | flops 1000000 | bytes 6000000 | tf_op jit(solution)/shard_map/split/pallas_call | solution.py:100
  10.1 12.6 %collective-permute-start.3 = (bf16[96,800]{1,0:T(8,128)(2,1)S(1)}, bf16[96,800]{1,0:T(8,128)(2,1)}, u32[]{:S(2)}, u32[]{:S(2)}) collective-permute-start(bf16[96,800]{1,0:T(8,128)(2,1)S(1)} %slice.18.upper_ref.refs_0_), channel_id=1, source_target_pairs={{0,30},{1,31},{2,0},{3,1},{4,2},{5,3},{6,4},{7,5},{8,6},{9,7},{10,... | collective-permute-start | bytes 460808 | tf_op jit(solution)/shard_map/ppermute | solution.py:362
  23.9 3.1 %collective-permute-start.4 = (bf16[104,800]{1,0:T(8,128)(2,1)S(1)}, bf16[104,800]{1,0:T(8,128)(2,1)}, u32[]{:S(2)}, u32[]{:S(2)}) collective-permute-start(bf16[104,800]{1,0:T(8,128)(2,1)S(1)} %slice.19.lower_ref.refs_1_), channel_id=1, source_target_pairs={{0,30},{1,31},{2,0},{3,1},{4,2},{5,3},{6,4},{7,5},{8,6},{9,7},{10,... | collective-permute-start | bytes 499208 | tf_op jit(solution)/shard_map/ppermute | solution.py:362
  27.6 3.2 %copy.9 = bf16[800,12,128]{0,2,1:T(8,128)(2,1)S(1)} copy(bf16[800,12,128]{2,0,1:T(8,128)(2,1)} %param.9) | data formatting | bytes 4915200 | tf_op args[3]
  31.5 3.4 %collective-permute-start.7 = (bf16[96,800]{1,0:T(8,128)(2,1)}, bf16[96,800]{1,0:T(8,128)(2,1)}, u32[]{:S(2)}, u32[]{:S(2)}) collective-permute-start(bf16[96,800]{1,0:T(8,128)(2,1)} %collective-permute-done.3.refs_4_), channel_id=1, source_target_pairs={{0,30},{1,31},{2,0},{3,1},{4,2},{5,3},{6,4},{7,5},{8,6},{9,7},{10,... | collective-permute-start | bytes 460808 | tf_op jit(solution)/shard_map/ppermute | solution.py:362
  35.4 2.7 %collective-permute-start.8 = (bf16[104,800]{1,0:T(8,128)(2,1)}, bf16[104,800]{1,0:T(8,128)(2,1)}, u32[]{:S(2)}, u32[]{:S(2)}) collective-permute-start(bf16[104,800]{1,0:T(8,128)(2,1)} %collective-permute-done.4.refs_5_), channel_id=1, source_target_pairs={{0,30},{1,31},{2,0},{3,1},{4,2},{5,3},{6,4},{7,5},{8,6},{9,7},{10,... | collective-permute-start | bytes 499208 | tf_op jit(solution)/shard_map/ppermute | solution.py:362
  38.2 1.4 copy-done
  39.6 2.9 %orbit.1 = (bf16[12,400,128]{2,1,0:T(8,128)(2,1)S(1)}, bf16[400,128]{1,0:T(8,128)(2,1)S(1)}, bf16[32,16,200]{2,1,0:T(8,128)(2,1)S(1)}) custom-call(s32[3]{0:T(128)S(1)} %pad_add_fusion.where_ref, bf16[200,800]{1,0:T(8,128)(2,1)} %own_ref.1, bf16[200,800]{1,0:T(8,128)(2,1)} %collective-permute-done.mate_ref, bf16[1536,800]{1,0:T(8,128)(2,1)S(1)} %bitcast.32, ...), custom_call_target="tpu_custom_call" | custom-call | flops 983040000 | bytes 6000000 | tf_op jit(solution)/shard_map/orbit/pallas_call | solution.py:72
  43.2 6.2 %exchange.9.before_ref = f32[12,8,200]{2,1,0:T(8,128)S(1)} custom-call(s32[2]{0:T(128)S(1)} %pad_add_fusion.3.where_ref, bf16[96,800]{1,0:T(8,128)(2,1)S(1)} %slice.18.upper_ref.refs_0_, bf16[104,800]{1,0:T(8,128)(2,1)S(1)} %slice.19.lower_ref.refs_1_, bf16[400,128]{1,0:T(8,128)(2,1)S(1)} %get-tuple-element.65.near_ref, ...), custom_call_target="tpu_custom_call" | custom-call | flops 983040000 | bytes 5000000 | tf_op jit(solution)/shard_map/exchange/pallas_call | solution.py:205
  49.4 6.6 %exchange.10.before_ref = f32[12,8,200]{2,1,0:T(8,128)S(1)} custom-call(s32[2]{0:T(128)S(1)} %pad_add_fusion.2.where_ref, bf16[96,800]{1,0:T(8,128)(2,1)} %collective-permute-done.1.upper_ref.refs_2_, bf16[104,800]{1,0:T(8,128)(2,1)S(1)} %collective-permute-done.2.lower_ref.refs_3_, bf16[400,128]{1,0:T(8,128)(2,1)S(1)} %get-tuple-element.65.near_ref, ...), custom_call_target="tpu_custom_call" | custom-call | flops 983040000 | bytes 5000000 | tf_op jit(solution)/shard_map/exchange/pallas_call | solution.py:205
  56.1 3.6 %collective-permute-start.12 = (bf16[96,800]{1,0:T(8,128)(2,1)}, bf16[96,800]{1,0:T(8,128)(2,1)}, u32[]{:S(2)}, u32[]{:S(2)}) collective-permute-start(bf16[96,800]{1,0:T(8,128)(2,1)} %collective-permute-done.7.upper_ref.refs_8_), channel_id=1, source_target_pairs={{0,30},{1,31},{2,0},{3,1},{4,2},{5,3},{6,4},{7,5},{8,6},{9,7},{10,... | collective-permute-start | bytes 460808 | tf_op jit(solution)/shard_map/ppermute | solution.py:362
  59.7 3.2 %collective-permute-start.13 = (bf16[104,800]{1,0:T(8,128)(2,1)}, bf16[104,800]{1,0:T(8,128)(2,1)}, u32[]{:S(2)}, u32[]{:S(2)}) collective-permute-start(bf16[104,800]{1,0:T(8,128)(2,1)} %collective-permute-done.8.lower_ref.refs_9_), channel_id=1, source_target_pairs={{0,30},{1,31},{2,0},{3,1},{4,2},{5,3},{6,4},{7,5},{8,6},{9,7},{10,... | collective-permute-start | bytes 499208 | tf_op jit(solution)/shard_map/ppermute | solution.py:362
  63.0 8.3 %all-to-all-start = ((bf16[32,16,200]{2,1,0:T(8,128)(2,1)}), bf16[32,16,200]{2,1,0:T(8,128)(2,1)}, u32[]{:S(2)}, u32[]{:S(2)}) async-start(bf16[32,16,200]{2,1,0:T(8,128)(2,1)} %copy-done.54), calls=%async_computation | async-start | bytes 524288 | tf_op jit(solution)/shard_map/all_to_all | solution.py:370
  71.3 1.4 copy-done.1
  72.8 1.4 copy-done.5
  74.2 1.3 copy-done.9
  75.5 6.7 %exchange.11.before_ref = f32[12,8,200]{2,1,0:T(8,128)S(1)} custom-call(s32[2]{0:T(128)S(1)} %pad_add_fusion.4.where_ref, bf16[96,800]{1,0:T(8,128)(2,1)} %collective-permute-done.7.upper_ref.refs_8_, bf16[104,800]{1,0:T(8,128)(2,1)} %collective-permute-done.8.lower_ref.refs_9_, bf16[400,128]{1,0:T(8,128)(2,1)S(1)} %get-tuple-element.65.near_ref, ...), custom_call_target="tpu_custom_call" | custom-call | flops 983040000 | bytes 5000000 | tf_op jit(solution)/shard_map/exchange/pallas_call | solution.py:205
  82.2 1.4 collective-permute-start.14
  83.7 2.0 collective-permute-start.16
  85.7 1.5 collective-permute-start.17
  87.8 6.7 %exchange.12.before_ref = f32[12,8,200]{2,1,0:T(8,128)S(1)} custom-call(s32[2]{0:T(128)S(1)} %pad_add_fusion.5.where_ref, bf16[96,800]{1,0:T(8,128)(2,1)} %collective-permute-done.10.upper_ref.refs_10_, bf16[104,800]{1,0:T(8,128)(2,1)} %collective-permute-done.11.lower_ref.refs_11_, bf16[400,128]{1,0:T(8,128)(2,1)S(1)} %get-tuple-element.65.near_ref, ...), custom_call_target="tpu_custom_call" | custom-call | flops 983040000 | bytes 5000000 | tf_op jit(solution)/shard_map/exchange/pallas_call | solution.py:205
  95.0 3.1 %collective-permute-start.20 = (bf16[96,800]{1,0:T(8,128)(2,1)S(1)}, bf16[96,800]{1,0:T(8,128)(2,1)S(1)}, u32[]{:S(2)}, u32[]{:S(2)}) collective-permute-start(bf16[96,800]{1,0:T(8,128)(2,1)S(1)} %collective-permute-done.16.upper_ref.refs_16_), channel_id=1, source_target_pairs={{0,30},{1,31},{2,0},{3,1},{4,2},{5,3},{6,4},{7,5},{8,6},{9,7},{10,... | collective-permute-start | bytes 460808 | tf_op jit(solution)/shard_map/ppermute | solution.py:362
  98.0 1.5 collective-permute-start.21
  100.1 6.2 %exchange.13.before_ref = f32[12,8,200]{2,1,0:T(8,128)S(1)} custom-call(s32[2]{0:T(128)S(1)} %pad_add_fusion.6.where_ref, bf16[96,800]{1,0:T(8,128)(2,1)S(1)} %collective-permute-done.16.upper_ref.refs_16_, bf16[104,800]{1,0:T(8,128)(2,1)S(1)} %collective-permute-done.17.lower_ref.refs_17_, bf16[400,128]{1,0:T(8,128)(2,1)S(1)} %get-tuple-element.65.near_ref, ...), custom_call_target="tpu_custom_call" | custom-call | flops 983040000 | bytes 5000000 | tf_op jit(solution)/shard_map/exchange/pallas_call | solution.py:205
  106.6 3.3 %collective-permute-start.24 = (bf16[96,800]{1,0:T(8,128)(2,1)S(1)}, bf16[96,800]{1,0:T(8,128)(2,1)S(1)}, u32[]{:S(2)}, u32[]{:S(2)}) collective-permute-start(bf16[96,800]{1,0:T(8,128)(2,1)S(1)} %collective-permute-done.20.refs_20_), channel_id=1, source_target_pairs={{0,30},{1,31},{2,0},{3,1},{4,2},{5,3},{6,4},{7,5},{8,6},{9,7},{10,... | collective-permute-start | bytes 460808 | tf_op jit(solution)/shard_map/ppermute | solution.py:362
  109.9 1.5 collective-permute-start.25
  111.4 13.6 %collective-permute-start.23 = (bf16[104,800]{1,0:T(8,128)(2,1)S(1)}, bf16[104,800]{1,0:T(8,128)(2,1)S(1)}, u32[]{:S(2)}, u32[]{:S(2)}) collective-permute-start(bf16[104,800]{1,0:T(8,128)(2,1)S(1)} %collective-permute-done.19.lower_ref.refs_19_), channel_id=1, source_target_pairs={{0,2},{1,3},{2,4},{3,5},{4,6},{5,7},{6,8},{7,9},{8,10},{9,11},{10,... | collective-permute-start | bytes 499208 | tf_op jit(solution)/shard_map/ppermute | solution.py:361
  125.7 6.2 %exchange.14.before_ref = f32[12,8,200]{2,1,0:T(8,128)S(1)} custom-call(s32[2]{0:T(128)S(1)} %pad_add_fusion.7.where_ref, bf16[96,800]{1,0:T(8,128)(2,1)S(1)} %collective-permute-done.18.upper_ref.refs_18_, bf16[104,800]{1,0:T(8,128)(2,1)S(1)} %collective-permute-done.19.lower_ref.refs_19_, bf16[400,128]{1,0:T(8,128)(2,1)S(1)} %get-tuple-element.65.near_ref, ...), custom_call_target="tpu_custom_call" | custom-call | flops 983040000 | bytes 5000000 | tf_op jit(solution)/shard_map/exchange/pallas_call | solution.py:205
  132.4 3.1 %collective-permute-start.28 = (bf16[96,800]{1,0:T(8,128)(2,1)S(1)}, bf16[96,800]{1,0:T(8,128)(2,1)S(1)}, u32[]{:S(2)}, u32[]{:S(2)}) collective-permute-start(bf16[96,800]{1,0:T(8,128)(2,1)S(1)} %collective-permute-done.24.upper_ref.refs_24_), channel_id=1, source_target_pairs={{0,30},{1,31},{2,0},{3,1},{4,2},{5,3},{6,4},{7,5},{8,6},{9,7},{10,... | collective-permute-start | bytes 460808 | tf_op jit(solution)/shard_map/ppermute | solution.py:362
  135.5 1.5 collective-permute-start.29
  137.6 6.2 %exchange.15.before_ref = f32[12,8,200]{2,1,0:T(8,128)S(1)} custom-call(s32[2]{0:T(128)S(1)} %pad_add_fusion.8.where_ref, bf16[96,800]{1,0:T(8,128)(2,1)S(1)} %collective-permute-done.24.upper_ref.refs_24_, bf16[104,800]{1,0:T(8,128)(2,1)S(1)} %collective-permute-done.25.lower_ref.refs_25_, bf16[400,128]{1,0:T(8,128)(2,1)S(1)} %get-tuple-element.65.near_ref, ...), custom_call_target="tpu_custom_call" | custom-call | flops 983040000 | bytes 5000000 | tf_op jit(solution)/shard_map/exchange/pallas_call | solution.py:205
  145.4 3.1 %collective-permute-start.31 = (bf16[104,800]{1,0:T(8,128)(2,1)}, bf16[104,800]{1,0:T(8,128)(2,1)}, u32[]{:S(2)}, u32[]{:S(2)}) collective-permute-start(bf16[104,800]{1,0:T(8,128)(2,1)} %collective-permute-done.29.refs_29_), channel_id=1, source_target_pairs={{0,30},{1,31},{2,0},{3,1},{4,2},{5,3},{6,4},{7,5},{8,6},{9,7},{10,... | collective-permute-start | bytes 499208 | tf_op jit(solution)/shard_map/ppermute | solution.py:406
  148.6 1.4 copy-done.6
  150.7 2.6 field.1
  153.9 11.6 %all-to-all-start.1 = ((f32[16,2,200]{2,1,0:T(2,128)}), f32[16,2,200]{2,1,0:T(2,128)S(1)}, u32[]{:S(2)}, u32[]{:S(2)}) async-start(f32[16,2,200]{2,1,0:T(2,128)} %copy-done.55), calls=%async_computation.1 | async-start | bytes 65536 | tf_op jit(solution)/shard_map/all_to_all | solution.py:374
  165.6 1.4 copy-done.2
  167.0 1.4 copy-done.7
  168.4 1.3 copy-done.10
  171.3 6.6 %exchange.16.before_ref = f32[12,8,200]{2,1,0:T(8,128)S(1)} custom-call(s32[2]{0:T(128)S(1)} %copy-done.56, bf16[96,800]{1,0:T(8,128)(2,1)} %collective-permute-done.26.upper_ref.refs_26_, bf16[104,800]{1,0:T(8,128)(2,1)S(1)} %copy-done.21, bf16[400,128]{1,0:T(8,128)(2,1)S(1)} %get-tuple-element.65.near_ref, f32[12,8,200]{2,1,0:T(8,128)S(1)} %exchange.15.before_ref, ...), custom_call_target="tpu_custom_call" | custom-call | flops 983040000 | bytes 5000000 | tf_op jit(solution)/shard_map/exchange/pallas_call | solution.py:205
  178.0 6.7 %exchange.17.refs_33_ = f32[12,8,200]{2,1,0:T(8,128)S(1)} custom-call(s32[2]{0:T(128)S(1)} %pad_add_fusion.9.where_ref, bf16[96,800]{1,0:T(8,128)(2,1)} %collective-permute-done.30.upper_ref.refs_30_, bf16[104,800]{1,0:T(8,128)(2,1)} %collective-permute-done.31.lower_ref.refs_31_, bf16[400,128]{1,0:T(8,128)(2,1)S(1)} %get-tuple-element.65.near_ref, ...), custom_call_target="tpu_custom_call" | custom-call | flops 983040000 | bytes 5000000 | tf_op jit(solution)/shard_map/exchange/pallas_call | solution.py:205
  198.6 12.5 %degree.3 = (f32[104,800]{1,0:T(8,128)S(1)}, f32[96,800]{1,0:T(8,128)S(1)}) custom-call(s32[17]{0:T(128)S(1)} %pad_add_fusion.1.where_ref, f32[16,2,200]{2,1,0:T(2,128)S(1)} %all-to-all-done.1.field_ref, bf16[96,800]{1,0:T(8,128)(2,1)S(1)} %slice.18.upper_ref.refs_0_, bf16[104,800]{1,0:T(8,128)(2,1)S(1)} %slice.19.lower_ref.refs_1_, ...), custom_call_target="tpu_custom_call" | custom-call | flops 983040000 | bytes 6000000 | tf_op jit(solution)/shard_map/degree/pallas_call | solution.py:286
  211.2 1.7 collective-permute-done.32.refs_33_
  213.0 12.4 %degree.4 = (f32[96,800]{1,0:T(8,128)S(1)}, f32[96,800]{1,0:T(8,128)S(1)}) custom-call(s32[17]{0:T(128)S(1)} %pad_add_fusion.1.where_ref, f32[16,2,200]{2,1,0:T(2,128)S(1)} %all-to-all-done.1.field_ref, bf16[96,800]{1,0:T(8,128)(2,1)S(1)} %slice.18.upper_ref.refs_0_, bf16[104,800]{1,0:T(8,128)(2,1)S(1)} %slice.19.lower_ref.refs_1_, ...), custom_call_target="tpu_custom_call" | custom-call | flops 983040000 | bytes 6000000 | tf_op jit(solution)/shard_map/degree/pallas_call | solution.py:286
  225.7 1.5 collective-permute-done.33.refs_33_
  227.2 12.3 %degree.5 = (f32[96,800]{1,0:T(8,128)S(1)}, f32[96,800]{1,0:T(8,128)S(1)}) custom-call(s32[17]{0:T(128)S(1)} %pad_add_fusion.1.where_ref, f32[16,2,200]{2,1,0:T(2,128)S(1)} %all-to-all-done.1.field_ref, bf16[96,800]{1,0:T(8,128)(2,1)S(1)} %slice.18.upper_ref.refs_0_, bf16[104,800]{1,0:T(8,128)(2,1)S(1)} %slice.19.lower_ref.refs_1_, ...), custom_call_target="tpu_custom_call" | custom-call | flops 983040000 | bytes 6000000 | tf_op jit(solution)/shard_map/degree/pallas_call | solution.py:286
  239.8 1.5 collective-permute-done.34.other_ref
  242.1 26.4 %all_to_all.15 = bf16[16,25,128]{2,1,0:T(8,128)(2,1)S(1)} all-to-all(bf16[16,25,128]{2,1,0:T(8,128)(2,1)S(1)} %finish.1), channel_id=1, replica_groups={{0,2,4,6,8,10,12,14,16,18,20,22,24,26,28,30},{1,3,5,7,9,11,13,15,17,19,..., dimensions={0} | all-to-all | bytes 204800 | tf_op jit(solution)/shard_map/all_to_all | solution.py:428
  (185 shorter events, 30.3 us)
Async XLA Ops:
  2.4 24.8 %copy-start.58 = (s32[16]{0:T(128)S(1)}, s32[16]{0:T(128)}, u32[]{:S(2)}) copy-start(s32[16]{0:T(128)} %constant.112.clone) | copy-start | bytes 196
  9.2 34.0 %collective-permute-start.9 = (bf16[16,200,200]{2,1,0:T(8,128)(2,1)}, bf16[16,200,200]{2,1,0:T(8,128)(2,1)}, u32[]{:S(2)}, u32[]{:S(2)}) collective-permute-start(bf16[16,200,200]{2,1,0:T(8,128)(2,1)} %get-tuple-element.63.away_ref), channel_id=1, source_target_pairs={{0,1},{1,0},{2,3},{3,2},{4,5},{5,4},{6,7},{7,6},{8,9},{9,8},{10,11... | collective-permute-start | bytes 3840008 | tf_op jit(solution)/shard_map/ppermute | solution.py:354
  10.1 17.2 %collective-permute-start.3 = (bf16[96,800]{1,0:T(8,128)(2,1)S(1)}, bf16[96,800]{1,0:T(8,128)(2,1)}, u32[]{:S(2)}, u32[]{:S(2)}) collective-permute-start(bf16[96,800]{1,0:T(8,128)(2,1)S(1)} %slice.18.upper_ref.refs_0_), channel_id=1, source_target_pairs={{0,30},{1,31},{2,0},{3,1},{4,2},{5,3},{6,4},{7,5},{8,6},{9,7},{10,... | collective-permute-start | bytes 460808 | tf_op jit(solution)/shard_map/ppermute | solution.py:362
  22.8 8.7 %collective-permute-start.1 = (bf16[96,800]{1,0:T(8,128)(2,1)S(1)}, bf16[96,800]{1,0:T(8,128)(2,1)}, u32[]{:S(2)}, u32[]{:S(2)}) collective-permute-start(bf16[96,800]{1,0:T(8,128)(2,1)S(1)} %slice.18.upper_ref.refs_0_), channel_id=1, source_target_pairs={{0,2},{1,3},{2,4},{3,5},{4,6},{5,7},{6,8},{7,9},{8,10},{9,11},{10,... | collective-permute-start | bytes 460808 | tf_op jit(solution)/shard_map/ppermute | solution.py:361
  22.8 15.4 %collective-permute-start = (bf16[200,800]{1,0:T(8,128)(2,1)}, bf16[200,800]{1,0:T(8,128)(2,1)}, u32[]{:S(2)}, u32[]{:S(2)}) collective-permute-start(bf16[200,800]{1,0:T(8,128)(2,1)} %own_ref.1), channel_id=1, source_target_pairs={{0,1},{1,0},{2,3},{3,2},{4,5},{5,4},{6,7},{7,6},{8,9},{9,8},{10,11... | collective-permute-start | bytes 960008 | tf_op jit(solution)/shard_map/ppermute | solution.py:354
  23.9 11.0 %collective-permute-start.4 = (bf16[104,800]{1,0:T(8,128)(2,1)S(1)}, bf16[104,800]{1,0:T(8,128)(2,1)}, u32[]{:S(2)}, u32[]{:S(2)}) collective-permute-start(bf16[104,800]{1,0:T(8,128)(2,1)S(1)} %slice.19.lower_ref.refs_1_), channel_id=1, source_target_pairs={{0,30},{1,31},{2,0},{3,1},{4,2},{5,3},{6,4},{7,5},{8,6},{9,7},{10,... | collective-permute-start | bytes 499208 | tf_op jit(solution)/shard_map/ppermute | solution.py:362
  27.4 8.1 %collective-permute-start.2 = (bf16[104,800]{1,0:T(8,128)(2,1)S(1)}, bf16[104,800]{1,0:T(8,128)(2,1)S(1)}, u32[]{:S(2)}, u32[]{:S(2)}) collective-permute-start(bf16[104,800]{1,0:T(8,128)(2,1)S(1)} %slice.19.lower_ref.refs_1_), channel_id=1, source_target_pairs={{0,2},{1,3},{2,4},{3,5},{4,6},{5,7},{6,8},{7,9},{8,10},{9,11},{10,... | collective-permute-start | bytes 499208 | tf_op jit(solution)/shard_map/ppermute | solution.py:361
  31.5 24.6 %collective-permute-start.7 = (bf16[96,800]{1,0:T(8,128)(2,1)}, bf16[96,800]{1,0:T(8,128)(2,1)}, u32[]{:S(2)}, u32[]{:S(2)}) collective-permute-start(bf16[96,800]{1,0:T(8,128)(2,1)} %collective-permute-done.3.refs_4_), channel_id=1, source_target_pairs={{0,30},{1,31},{2,0},{3,1},{4,2},{5,3},{6,4},{7,5},{8,6},{9,7},{10,... | collective-permute-start | bytes 460808 | tf_op jit(solution)/shard_map/ppermute | solution.py:362
  34.9 21.2 %collective-permute-start.5 = (bf16[96,800]{1,0:T(8,128)(2,1)}, bf16[96,800]{1,0:T(8,128)(2,1)}, u32[]{:S(2)}, u32[]{:S(2)}) collective-permute-start(bf16[96,800]{1,0:T(8,128)(2,1)} %collective-permute-done.1.upper_ref.refs_2_), channel_id=1, source_target_pairs={{0,2},{1,3},{2,4},{3,5},{4,6},{5,7},{6,8},{7,9},{8,10},{9,11},{10,... | collective-permute-start | bytes 460808 | tf_op jit(solution)/shard_map/ppermute | solution.py:361
  35.4 20.7 %collective-permute-start.8 = (bf16[104,800]{1,0:T(8,128)(2,1)}, bf16[104,800]{1,0:T(8,128)(2,1)}, u32[]{:S(2)}, u32[]{:S(2)}) collective-permute-start(bf16[104,800]{1,0:T(8,128)(2,1)} %collective-permute-done.4.refs_5_), channel_id=1, source_target_pairs={{0,30},{1,31},{2,0},{3,1},{4,2},{5,3},{6,4},{7,5},{8,6},{9,7},{10,... | collective-permute-start | bytes 499208 | tf_op jit(solution)/shard_map/ppermute | solution.py:362
  38.1 17.9 %collective-permute-start.6 = (bf16[104,800]{1,0:T(8,128)(2,1)S(1)}, bf16[104,800]{1,0:T(8,128)(2,1)}, u32[]{:S(2)}, u32[]{:S(2)}) collective-permute-start(bf16[104,800]{1,0:T(8,128)(2,1)S(1)} %collective-permute-done.2.lower_ref.refs_3_), channel_id=1, source_target_pairs={{0,2},{1,3},{2,4},{3,5},{4,6},{5,7},{6,8},{7,9},{8,10},{9,11},{10,... | collective-permute-start | bytes 499208 | tf_op jit(solution)/shard_map/ppermute | solution.py:361
  56.1 27.5 %collective-permute-start.12 = (bf16[96,800]{1,0:T(8,128)(2,1)}, bf16[96,800]{1,0:T(8,128)(2,1)}, u32[]{:S(2)}, u32[]{:S(2)}) collective-permute-start(bf16[96,800]{1,0:T(8,128)(2,1)} %collective-permute-done.7.upper_ref.refs_8_), channel_id=1, source_target_pairs={{0,30},{1,31},{2,0},{3,1},{4,2},{5,3},{6,4},{7,5},{8,6},{9,7},{10,... | collective-permute-start | bytes 460808 | tf_op jit(solution)/shard_map/ppermute | solution.py:362
  59.7 22.5 %collective-permute-start.10 = (bf16[96,800]{1,0:T(8,128)(2,1)}, bf16[96,800]{1,0:T(8,128)(2,1)}, u32[]{:S(2)}, u32[]{:S(2)}) collective-permute-start(bf16[96,800]{1,0:T(8,128)(2,1)} %collective-permute-done.5.refs_6_), channel_id=1, source_target_pairs={{0,2},{1,3},{2,4},{3,5},{4,6},{5,7},{6,8},{7,9},{8,10},{9,11},{10,... | collective-permute-start | bytes 460808 | tf_op jit(solution)/shard_map/ppermute | solution.py:361
  59.7 23.9 %collective-permute-start.13 = (bf16[104,800]{1,0:T(8,128)(2,1)}, bf16[104,800]{1,0:T(8,128)(2,1)}, u32[]{:S(2)}, u32[]{:S(2)}) collective-permute-start(bf16[104,800]{1,0:T(8,128)(2,1)} %collective-permute-done.8.lower_ref.refs_9_), channel_id=1, source_target_pairs={{0,30},{1,31},{2,0},{3,1},{4,2},{5,3},{6,4},{7,5},{8,6},{9,7},{10,... | collective-permute-start | bytes 499208 | tf_op jit(solution)/shard_map/ppermute | solution.py:362
  63.0 20.7 %collective-permute-start.11 = (bf16[104,800]{1,0:T(8,128)(2,1)}, bf16[104,800]{1,0:T(8,128)(2,1)}, u32[]{:S(2)}, u32[]{:S(2)}) collective-permute-start(bf16[104,800]{1,0:T(8,128)(2,1)} %collective-permute-done.6.refs_7_), channel_id=1, source_target_pairs={{0,2},{1,3},{2,4},{3,5},{4,6},{5,7},{6,8},{7,9},{8,10},{9,11},{10,... | collective-permute-start | bytes 499208 | tf_op jit(solution)/shard_map/ppermute | solution.py:361
  63.0 85.5 %all-to-all-start = ((bf16[32,16,200]{2,1,0:T(8,128)(2,1)}), bf16[32,16,200]{2,1,0:T(8,128)(2,1)}, u32[]{:S(2)}, u32[]{:S(2)}) async-start(bf16[32,16,200]{2,1,0:T(8,128)(2,1)} %copy-done.54), calls=%async_computation | async-start | bytes 524288 | tf_op jit(solution)/shard_map/all_to_all | solution.py:370
  82.2 12.3 %collective-permute-start.14 = (bf16[96,800]{1,0:T(8,128)(2,1)}, bf16[96,800]{1,0:T(8,128)(2,1)S(1)}, u32[]{:S(2)}, u32[]{:S(2)}) collective-permute-start(bf16[96,800]{1,0:T(8,128)(2,1)} %collective-permute-done.10.upper_ref.refs_10_), channel_id=1, source_target_pairs={{0,2},{1,3},{2,4},{3,5},{4,6},{5,7},{6,8},{7,9},{8,10},{9,11},{10,... | collective-permute-start | bytes 460808 | tf_op jit(solution)/shard_map/ppermute | solution.py:361
  83.7 11.3 %collective-permute-start.16 = (bf16[96,800]{1,0:T(8,128)(2,1)}, bf16[96,800]{1,0:T(8,128)(2,1)S(1)}, u32[]{:S(2)}, u32[]{:S(2)}) collective-permute-start(bf16[96,800]{1,0:T(8,128)(2,1)} %collective-permute-done.12.refs_12_), channel_id=1, source_target_pairs={{0,30},{1,31},{2,0},{3,1},{4,2},{5,3},{6,4},{7,5},{8,6},{9,7},{10,... | collective-permute-start | bytes 460808 | tf_op jit(solution)/shard_map/ppermute | solution.py:362
  85.7 9.3 %collective-permute-start.17 = (bf16[104,800]{1,0:T(8,128)(2,1)}, bf16[104,800]{1,0:T(8,128)(2,1)S(1)}, u32[]{:S(2)}, u32[]{:S(2)}) collective-permute-start(bf16[104,800]{1,0:T(8,128)(2,1)} %collective-permute-done.13.refs_13_), channel_id=1, source_target_pairs={{0,30},{1,31},{2,0},{3,1},{4,2},{5,3},{6,4},{7,5},{8,6},{9,7},{10,... | collective-permute-start | bytes 499208 | tf_op jit(solution)/shard_map/ppermute | solution.py:362
  87.2 7.7 %collective-permute-start.15 = (bf16[104,800]{1,0:T(8,128)(2,1)}, bf16[104,800]{1,0:T(8,128)(2,1)S(1)}, u32[]{:S(2)}, u32[]{:S(2)}) collective-permute-start(bf16[104,800]{1,0:T(8,128)(2,1)} %collective-permute-done.11.lower_ref.refs_11_), channel_id=1, source_target_pairs={{0,2},{1,3},{2,4},{3,5},{4,6},{5,7},{6,8},{7,9},{8,10},{9,11},{10,... | collective-permute-start | bytes 499208 | tf_op jit(solution)/shard_map/ppermute | solution.py:361
  94.5 11.9 %collective-permute-start.18 = (bf16[96,800]{1,0:T(8,128)(2,1)S(1)}, bf16[96,800]{1,0:T(8,128)(2,1)S(1)}, u32[]{:S(2)}, u32[]{:S(2)}) collective-permute-start(bf16[96,800]{1,0:T(8,128)(2,1)S(1)} %collective-permute-done.14.refs_14_), channel_id=1, source_target_pairs={{0,2},{1,3},{2,4},{3,5},{4,6},{5,7},{6,8},{7,9},{8,10},{9,11},{10,... | collective-permute-start | bytes 460808 | tf_op jit(solution)/shard_map/ppermute | solution.py:361
  95.0 11.6 %collective-permute-start.20 = (bf16[96,800]{1,0:T(8,128)(2,1)S(1)}, bf16[96,800]{1,0:T(8,128)(2,1)S(1)}, u32[]{:S(2)}, u32[]{:S(2)}) collective-permute-start(bf16[96,800]{1,0:T(8,128)(2,1)S(1)} %collective-permute-done.16.upper_ref.refs_16_), channel_id=1, source_target_pairs={{0,30},{1,31},{2,0},{3,1},{4,2},{5,3},{6,4},{7,5},{8,6},{9,7},{10,... | collective-permute-start | bytes 460808 | tf_op jit(solution)/shard_map/ppermute | solution.py:362
  98.0 8.6 %collective-permute-start.21 = (bf16[104,800]{1,0:T(8,128)(2,1)S(1)}, bf16[104,800]{1,0:T(8,128)(2,1)S(1)}, u32[]{:S(2)}, u32[]{:S(2)}) collective-permute-start(bf16[104,800]{1,0:T(8,128)(2,1)S(1)} %collective-permute-done.17.lower_ref.refs_17_), channel_id=1, source_target_pairs={{0,30},{1,31},{2,0},{3,1},{4,2},{5,3},{6,4},{7,5},{8,6},{9,7},{10,... | collective-permute-start | bytes 499208 | tf_op jit(solution)/shard_map/ppermute | solution.py:362
  99.6 7.0 %collective-permute-start.19 = (bf16[104,800]{1,0:T(8,128)(2,1)S(1)}, bf16[104,800]{1,0:T(8,128)(2,1)S(1)}, u32[]{:S(2)}, u32[]{:S(2)}) collective-permute-start(bf16[104,800]{1,0:T(8,128)(2,1)S(1)} %collective-permute-done.15.refs_15_), channel_id=1, source_target_pairs={{0,2},{1,3},{2,4},{3,5},{4,6},{5,7},{6,8},{7,9},{8,10},{9,11},{10,... | collective-permute-start | bytes 499208 | tf_op jit(solution)/shard_map/ppermute | solution.py:361
  106.4 25.5 %copy-start.27 = (bf16[96,800]{1,0:T(8,128)(2,1)}, bf16[96,800]{1,0:T(8,128)(2,1)S(1)}, u32[]{:S(2)}) copy-start(bf16[96,800]{1,0:T(8,128)(2,1)S(1)} %collective-permute-done.18.upper_ref.refs_18_) | copy-start | bytes 460804
  106.4 25.5 %collective-permute-start.22 = (bf16[96,800]{1,0:T(8,128)(2,1)S(1)}, bf16[96,800]{1,0:T(8,128)(2,1)S(1)}, u32[]{:S(2)}, u32[]{:S(2)}) collective-permute-start(bf16[96,800]{1,0:T(8,128)(2,1)S(1)} %collective-permute-done.18.upper_ref.refs_18_), channel_id=1, source_target_pairs={{0,2},{1,3},{2,4},{3,5},{4,6},{5,7},{6,8},{7,9},{8,10},{9,11},{10,... | collective-permute-start | bytes 460808 | tf_op jit(solution)/shard_map/ppermute | solution.py:361
  106.6 25.4 %copy-start.14 = (bf16[104,800]{1,0:T(8,128)(2,1)}, bf16[104,800]{1,0:T(8,128)(2,1)S(1)}, u32[]{:S(2)}) copy-start(bf16[104,800]{1,0:T(8,128)(2,1)S(1)} %collective-permute-done.19.lower_ref.refs_19_) | copy-start | bytes 499204
  106.6 25.4 %copy-start.44 = (bf16[96,800]{1,0:T(8,128)(2,1)}, bf16[96,800]{1,0:T(8,128)(2,1)S(1)}, u32[]{:S(2)}) copy-start(bf16[96,800]{1,0:T(8,128)(2,1)S(1)} %collective-permute-done.20.refs_20_) | copy-start | bytes 460804
  106.6 25.4 %copy-start.35 = (bf16[104,800]{1,0:T(8,128)(2,1)}, bf16[104,800]{1,0:T(8,128)(2,1)S(1)}, u32[]{:S(2)}) copy-start(bf16[104,800]{1,0:T(8,128)(2,1)S(1)} %collective-permute-done.21.refs_21_) | copy-start | bytes 499204
  106.6 25.7 %collective-permute-start.24 = (bf16[96,800]{1,0:T(8,128)(2,1)S(1)}, bf16[96,800]{1,0:T(8,128)(2,1)S(1)}, u32[]{:S(2)}, u32[]{:S(2)}) collective-permute-start(bf16[96,800]{1,0:T(8,128)(2,1)S(1)} %collective-permute-done.20.refs_20_), channel_id=1, source_target_pairs={{0,30},{1,31},{2,0},{3,1},{4,2},{5,3},{6,4},{7,5},{8,6},{9,7},{10,... | collective-permute-start | bytes 460808 | tf_op jit(solution)/shard_map/ppermute | solution.py:362
  109.9 22.5 %collective-permute-start.25 = (bf16[104,800]{1,0:T(8,128)(2,1)S(1)}, bf16[104,800]{1,0:T(8,128)(2,1)S(1)}, u32[]{:S(2)}, u32[]{:S(2)}) collective-permute-start(bf16[104,800]{1,0:T(8,128)(2,1)S(1)} %collective-permute-done.21.refs_21_), channel_id=1, source_target_pairs={{0,30},{1,31},{2,0},{3,1},{4,2},{5,3},{6,4},{7,5},{8,6},{9,7},{10,... | collective-permute-start | bytes 499208 | tf_op jit(solution)/shard_map/ppermute | solution.py:362
  111.4 20.9 %collective-permute-start.23 = (bf16[104,800]{1,0:T(8,128)(2,1)S(1)}, bf16[104,800]{1,0:T(8,128)(2,1)S(1)}, u32[]{:S(2)}, u32[]{:S(2)}) collective-permute-start(bf16[104,800]{1,0:T(8,128)(2,1)S(1)} %collective-permute-done.19.lower_ref.refs_19_), channel_id=1, source_target_pairs={{0,2},{1,3},{2,4},{3,5},{4,6},{5,7},{6,8},{7,9},{8,10},{9,11},{10,... | collective-permute-start | bytes 499208 | tf_op jit(solution)/shard_map/ppermute | solution.py:361
  132.0 11.9 %collective-permute-start.26 = (bf16[96,800]{1,0:T(8,128)(2,1)S(1)}, bf16[96,800]{1,0:T(8,128)(2,1)}, u32[]{:S(2)}, u32[]{:S(2)}) collective-permute-start(bf16[96,800]{1,0:T(8,128)(2,1)S(1)} %collective-permute-done.22.refs_22_), channel_id=1, source_target_pairs={{0,2},{1,3},{2,4},{3,5},{4,6},{5,7},{6,8},{7,9},{8,10},{9,11},{10,... | collective-permute-start | bytes 460808 | tf_op jit(solution)/shard_map/ppermute | solution.py:361
  132.4 12.4 %collective-permute-start.28 = (bf16[96,800]{1,0:T(8,128)(2,1)S(1)}, bf16[96,800]{1,0:T(8,128)(2,1)S(1)}, u32[]{:S(2)}, u32[]{:S(2)}) collective-permute-start(bf16[96,800]{1,0:T(8,128)(2,1)S(1)} %collective-permute-done.24.upper_ref.refs_24_), channel_id=1, source_target_pairs={{0,30},{1,31},{2,0},{3,1},{4,2},{5,3},{6,4},{7,5},{8,6},{9,7},{10,... | collective-permute-start | bytes 460808 | tf_op jit(solution)/shard_map/ppermute | solution.py:362
  135.5 10.0 %collective-permute-start.29 = (bf16[104,800]{1,0:T(8,128)(2,1)S(1)}, bf16[104,800]{1,0:T(8,128)(2,1)}, u32[]{:S(2)}, u32[]{:S(2)}) collective-permute-start(bf16[104,800]{1,0:T(8,128)(2,1)S(1)} %collective-permute-done.25.lower_ref.refs_25_), channel_id=1, source_target_pairs={{0,30},{1,31},{2,0},{3,1},{4,2},{5,3},{6,4},{7,5},{8,6},{9,7},{10,... | collective-permute-start | bytes 499208 | tf_op jit(solution)/shard_map/ppermute | solution.py:362
  137.0 7.1 %collective-permute-start.27 = (bf16[104,800]{1,0:T(8,128)(2,1)S(1)}, bf16[104,800]{1,0:T(8,128)(2,1)S(1)}, u32[]{:S(2)}, u32[]{:S(2)}) collective-permute-start(bf16[104,800]{1,0:T(8,128)(2,1)S(1)} %collective-permute-done.23.refs_23_), channel_id=1, source_target_pairs={{0,2},{1,3},{2,4},{3,5},{4,6},{5,7},{6,8},{7,9},{8,10},{9,11},{10,... | collective-permute-start | bytes 499208 | tf_op jit(solution)/shard_map/ppermute | solution.py:361
  143.9 34.1 %collective-permute-start.30 = (bf16[96,800]{1,0:T(8,128)(2,1)}, bf16[96,800]{1,0:T(8,128)(2,1)}, u32[]{:S(2)}, u32[]{:S(2)}) collective-permute-start(bf16[96,800]{1,0:T(8,128)(2,1)} %collective-permute-done.26.upper_ref.refs_26_), channel_id=1, source_target_pairs={{0,2},{1,3},{2,4},{3,5},{4,6},{5,7},{6,8},{7,9},{8,10},{9,11},{10,... | collective-permute-start | bytes 460808 | tf_op jit(solution)/shard_map/ppermute | solution.py:406
  145.4 32.5 %collective-permute-start.31 = (bf16[104,800]{1,0:T(8,128)(2,1)}, bf16[104,800]{1,0:T(8,128)(2,1)}, u32[]{:S(2)}, u32[]{:S(2)}) collective-permute-start(bf16[104,800]{1,0:T(8,128)(2,1)} %collective-permute-done.29.refs_29_), channel_id=1, source_target_pairs={{0,30},{1,31},{2,0},{3,1},{4,2},{5,3},{6,4},{7,5},{8,6},{9,7},{10,... | collective-permute-start | bytes 499208 | tf_op jit(solution)/shard_map/ppermute | solution.py:406
  153.9 30.8 %all-to-all-start.1 = ((f32[16,2,200]{2,1,0:T(2,128)}), f32[16,2,200]{2,1,0:T(2,128)S(1)}, u32[]{:S(2)}, u32[]{:S(2)}) async-start(f32[16,2,200]{2,1,0:T(2,128)} %copy-done.55), calls=%async_computation.1 | async-start | bytes 65536 | tf_op jit(solution)/shard_map/all_to_all | solution.py:374
  198.5 14.4 %copy-start.26 = (bf16[96,800]{1,0:T(8,128)(2,1)S(1)}, bf16[96,800]{1,0:T(8,128)(2,1)}, u32[]{:S(2)}) copy-start(bf16[96,800]{1,0:T(8,128)(2,1)} %copy-done.24) | copy-start | bytes 460804
  198.5 14.4 %copy-start.34 = (bf16[104,800]{1,0:T(8,128)(2,1)S(1)}, bf16[104,800]{1,0:T(8,128)(2,1)}, u32[]{:S(2)}) copy-start(bf16[104,800]{1,0:T(8,128)(2,1)} %copy-done.32) | copy-start | bytes 499204
  198.6 14.4 %copy-start.37 = (bf16[104,800]{1,0:T(8,128)(2,1)S(1)}, bf16[104,800]{1,0:T(8,128)(2,1)}, u32[]{:S(2)}) copy-start(bf16[104,800]{1,0:T(8,128)(2,1)} %copy-done.35) | copy-start | bytes 499204
  198.6 14.4 %copy-start.40 = (bf16[104,800]{1,0:T(8,128)(2,1)S(1)}, bf16[104,800]{1,0:T(8,128)(2,1)}, u32[]{:S(2)}) copy-start(bf16[104,800]{1,0:T(8,128)(2,1)} %copy-done.38) | copy-start | bytes 499204
  198.6 14.4 %copy-start.43 = (bf16[96,800]{1,0:T(8,128)(2,1)S(1)}, bf16[96,800]{1,0:T(8,128)(2,1)}, u32[]{:S(2)}) copy-start(bf16[96,800]{1,0:T(8,128)(2,1)} %copy-done.41) | copy-start | bytes 460804
  198.6 14.4 %copy-start.46 = (bf16[96,800]{1,0:T(8,128)(2,1)S(1)}, bf16[96,800]{1,0:T(8,128)(2,1)}, u32[]{:S(2)}) copy-start(bf16[96,800]{1,0:T(8,128)(2,1)} %copy-done.44) | copy-start | bytes 460804
  211.1 1.8 collective-permute-start.32
  225.4 1.8 collective-permute-start.33
  239.5 1.8 collective-permute-start.34
  (48 other events, 221.4 us)
